TPU v7x, 32 devices: a whole 2x2x4 slice. The times are simulated.
32 devices in a mesh: dp: 8 (over z, y), fsdp: 4 (over x, core).
Axes of the slice: x: 2, y: 2, z: 4, core: 2. Of those that a mesh axis runs over, the one named last changes fastest.
Arguments:
- hidden_in: bfloat16 [2, 32, 256, 768], P(None, ('dp', 'fsdp')), may hold values from -6 to 6
- patches: bfloat16 [2, 32, 2048, 768], P(None, ('dp', 'fsdp')), may hold values from -6 to 6
- token_segments: int32 [2, 32, 256], P(None, ('dp', 'fsdp')), may hold values from 0 to 3, as said below
- patch_segments: int32 [2, 32, 2048], P(None, ('dp', 'fsdp')), may hold values from 0 to 3, as said below
- cotangent: bfloat16 [2, 32, 256, 768], P(None, ('dp', 'fsdp')), may hold values from -6 to 6
- attention_weights: float32 [8, 768, 768], P(None, 'fsdp', 'dp'), may hold values from -1.1547005 to 1.1547005
- attention_means: float32 [8, 768, 768], P(None, 'fsdp', 'dp'), may hold values from -40 to 40
- attention_squares: float32 [8, 768, 768], P(None, 'fsdp', 'dp'), may hold values from 131.072 to 1638.4
- inner_weights: float32 [2, 768, 2048], P(None, 'fsdp', 'dp'), may hold values from -0.21875 to 0.21875
- inner_means: float32 [2, 768, 2048], P(None, 'fsdp', 'dp'), may hold values from -40 to 40
- inner_squares: float32 [2, 768, 2048], P(None, 'fsdp', 'dp'), may hold values from 131.072 to 1638.4
- outer_weights: float32 [2048, 768], P('fsdp', 'dp'), may hold values from -0.125 to 0.125
- outer_means: float32 [2048, 768], P('fsdp', 'dp'), may hold values from -48 to 48
- outer_squares: float32 [2048, 768], P('fsdp', 'dp'), may hold values from 163.84 to 2457.6
- norm_gains: float32 [3, 768], P(None, 'fsdp'), may hold values from 0.25 to 1.75
- gain_means: float32 [3, 768], P(None, 'fsdp'), may hold values from -80 to 80
- gain_squares: float32 [3, 768], P(None, 'fsdp'), may hold values from 425.984 to 6881.28
Outputs:
- hidden_out: bfloat16 [2, 32, 256, 768], P(None, ('dp', 'fsdp'))
- hidden_grad: float32 [2, 32, 256, 768], P(None, ('dp', 'fsdp'))
- patch_grad: float32 [2, 32, 2048, 768], P(None, ('dp', 'fsdp'))
- attention_mean: float32 [8, 768, 768], P(None, 'fsdp', 'dp')
- attention_square: float32 [8, 768, 768], P(None, 'fsdp', 'dp')
- attention_master: float32 [8, 768, 768], P(None, 'fsdp', 'dp')
- attention_copy: bfloat16 [8, 768, 768], P(None, 'fsdp', 'dp')
- inner_mean: float32 [2, 768, 2048], P(None, 'fsdp', 'dp')
- inner_square: float32 [2, 768, 2048], P(None, 'fsdp', 'dp')
- inner_master: float32 [2, 768, 2048], P(None, 'fsdp', 'dp')
- inner_copy: bfloat16 [2, 768, 2048], P(None, 'fsdp', 'dp')
- outer_mean: float32 [2048, 768], P('fsdp', 'dp')
- outer_square: float32 [2048, 768], P('fsdp', 'dp')
- outer_master: float32 [2048, 768], P('fsdp', 'dp')
- outer_copy: bfloat16 [2048, 768], P('fsdp', 'dp')
- gain_mean: float32 [3, 768], P(None, 'fsdp')
- gain_square: float32 [3, 768], P(None, 'fsdp')
- gain_master: float32 [3, 768], P(None, 'fsdp')
- gain_copy: bfloat16 [3, 768], P(None, 'fsdp')
Inputs may be any that keep to these rules, and one draw needn't show every extreme that they name: `token_segments`: along each row the ids never fall from one token to the next, and each of the 4 ids holds one token or more. `patch_segments`: along each row the ids never fall from one patch to the next, and each of the 4 ids holds one patch or more.
All inputs are finite; a program needn't handle non-finite values.
Results may differ from a plain program's by a relative error of at most 0.02.
The roundings to bfloat16 on the way count: a program that leaves them out, or rounds other values in their place, can miss the bound.
Values may be sent and summed in bfloat16 or wider, within the bound.
A program may use at most 320 MiB of HBM per device.

v0:
```python
import jax
import jax.numpy as jnp
from jax import lax
from jax.sharding import PartitionSpec as P

D = 768
HEADS = 12
HEAD = 64
STEP = 10
epsilon = 1e-06
score_scale = 0.125
masked_value = -1000000000.0
beta_one = 0.9
beta_two = 0.95
adam_epsilon = 1e-08
decay_matrix = 0.1
rate_matrix = 0.1
rate_gain = 0.3
float_type = jnp.float32
brain_type = jnp.bfloat16


def gelu_tanh(values):
    return (
        0.5
        * values
        * (1.0 + jnp.tanh(0.7978845608028654 * (values + 0.044715 * values * values * values)))
    )


def split_heads(matrix):
    return matrix.reshape(matrix.shape[:-1] + (HEADS, HEAD))


def norm_forward(values, gain):
    inverse_rms = lax.rsqrt(jnp.mean(values * values, axis=-1, keepdims=True) + epsilon)
    unit_rows = values * inverse_rms
    return (unit_rows * gain.astype(float_type), unit_rows, inverse_rms)


def norm_backward(grad_rows, gain, unit_rows, inverse_rms):
    grad_unit = grad_rows * gain.astype(float_type)
    grad_values = inverse_rms * (
        grad_unit - unit_rows * jnp.mean(grad_unit * unit_rows, axis=-1, keepdims=True)
    )
    return (grad_values, jnp.sum(grad_rows * unit_rows, axis=0))


def softmax_rows(scores):
    row_maximum = jnp.max(scores, axis=-1, keepdims=True)
    raised = jnp.exp(scores - row_maximum)
    return raised / jnp.sum(raised, axis=-1, keepdims=True)


def attend_forward(queries, key_heads, value_heads, allowed):
    scores = score_scale * jnp.einsum(
        "qhe,khe->hqk", queries, key_heads, preferred_element_type=float_type
    )
    probabilities = softmax_rows(jnp.where(allowed[None], scores, masked_value))
    rounded_probs = probabilities.astype(brain_type)
    mixture = jnp.einsum(
        "hqk,khe->qhe", rounded_probs, value_heads, preferred_element_type=float_type
    )
    return (mixture.astype(brain_type), probabilities, rounded_probs)


def attend_backward(grad_mixture, queries, key_heads, value_heads, probabilities, rounded_probs):
    grad_probs = jnp.einsum(
        "qhe,khe->hqk", grad_mixture, value_heads, preferred_element_type=float_type
    )
    grad_values = jnp.einsum(
        "hqk,qhe->khe", rounded_probs, grad_mixture, preferred_element_type=float_type
    ).astype(brain_type)
    row_inner = jnp.sum(probabilities * grad_probs, axis=-1, keepdims=True)
    grad_scores = (probabilities * (grad_probs - row_inner)).astype(brain_type)
    grad_queries = (
        score_scale
        * jnp.einsum("hqk,khe->qhe", grad_scores, key_heads, preferred_element_type=float_type)
    ).astype(brain_type)
    grad_keys = (
        score_scale
        * jnp.einsum("hqk,qhe->khe", grad_scores, queries, preferred_element_type=float_type)
    ).astype(brain_type)
    return (grad_queries, grad_keys, grad_values)


def layer_forward(weights, hidden, patch_rows, token_ids, patch_ids):
    attention, inner_matrix, outer_matrix, gain_rows = weights
    length = hidden.shape[0]
    initial = hidden.astype(float_type)
    normed_one, unit_one, rms_one = norm_forward(initial, gain_rows[0])
    normed_one = normed_one.astype(brain_type)
    projected = jnp.einsum(
        "nd,kde->kne", normed_one, attention[0:3], preferred_element_type=float_type
    ).astype(brain_type)
    heads_in = split_heads(projected)
    places = jnp.arange(length)
    causal = (places[:, None] >= places[None, :]) & (token_ids[:, None] == token_ids[None, :])
    mixture_one, probs_one, rounded_one = attend_forward(
        heads_in[0], heads_in[1], heads_in[2], causal
    )
    mixture_one = mixture_one.reshape(length, D)
    after_one = initial + jnp.dot(mixture_one, attention[3], preferred_element_type=float_type)
    normed_two, unit_two, rms_two = norm_forward(after_one, gain_rows[1])
    normed_two = normed_two.astype(brain_type)
    cross_query = split_heads(
        jnp.dot(normed_two, attention[4], preferred_element_type=float_type).astype(brain_type)
    )
    cross_pair = split_heads(
        jnp.einsum(
            "pd,kde->kpe", patch_rows, attention[5:7], preferred_element_type=float_type
        ).astype(brain_type)
    )
    matching = token_ids[:, None] == patch_ids[None, :]
    mixture_two, probs_two, rounded_two = attend_forward(
        cross_query, cross_pair[0], cross_pair[1], matching
    )
    mixture_two = mixture_two.reshape(length, D)
    after_two = after_one + jnp.dot(mixture_two, attention[7], preferred_element_type=float_type)
    normed_three, unit_three, rms_three = norm_forward(after_two, gain_rows[2])
    normed_three = normed_three.astype(brain_type)
    gated = jnp.einsum("nd,kdf->knf", normed_three, inner_matrix, preferred_element_type=float_type)
    units = (gelu_tanh(gated[0]) * gated[1]).astype(brain_type)
    layer_out = (
        after_two + jnp.dot(units, outer_matrix, preferred_element_type=float_type)
    ).astype(brain_type)
    stored = {
        "unit_one": unit_one,
        "rms_one": rms_one,
        "normed_one": normed_one,
        "heads_in": heads_in,
        "probs_one": probs_one,
        "rounded_one": rounded_one,
        "mixture_one": mixture_one,
        "unit_two": unit_two,
        "rms_two": rms_two,
        "normed_two": normed_two,
        "cross_query": cross_query,
        "cross_pair": cross_pair,
        "probs_two": probs_two,
        "rounded_two": rounded_two,
        "mixture_two": mixture_two,
        "unit_three": unit_three,
        "rms_three": rms_three,
        "normed_three": normed_three,
        "gated": gated,
        "units": units,
    }
    return (layer_out, stored)


def layer_backward(weights, stored, cotangent_row, patch_rows):
    attention, inner_matrix, outer_matrix, gain_rows = weights
    length = cotangent_row.shape[0]
    grad_final = cotangent_row.astype(float_type)
    grad_low = grad_final.astype(brain_type)
    grad_outer = jnp.einsum(
        "nf,nd->fd", stored["units"], grad_low, preferred_element_type=float_type
    )
    grad_units = jnp.einsum("nd,fd->nf", grad_low, outer_matrix, preferred_element_type=float_type)
    gate_in = stored["gated"][0]
    up_in = stored["gated"][1]
    activation, gelu_back = jax.vjp(gelu_tanh, gate_in)
    grad_gate = gelu_back(grad_units * up_in)[0]
    grad_gated = jnp.stack([grad_gate, grad_units * activation]).astype(brain_type)
    grad_inner = jnp.einsum(
        "nd,knf->kdf", stored["normed_three"], grad_gated, preferred_element_type=float_type
    )
    grad_normed = jnp.einsum(
        "knf,kdf->nd", grad_gated, inner_matrix, preferred_element_type=float_type
    )
    grad_from_three, gain_three = norm_backward(
        grad_normed, gain_rows[2], stored["unit_three"], stored["rms_three"]
    )
    grad_after_two = grad_final + grad_from_three
    branch_two = grad_after_two.astype(brain_type)
    grad_cross_out = jnp.einsum(
        "nd,ne->de", stored["mixture_two"], branch_two, preferred_element_type=float_type
    )
    grad_mixture_two = split_heads(
        jnp.einsum("ne,de->nd", branch_two, attention[7], preferred_element_type=float_type).astype(
            brain_type
        )
    )
    cross_pair = stored["cross_pair"]
    grad_cq, grad_ck, grad_cv = attend_backward(
        grad_mixture_two,
        stored["cross_query"],
        cross_pair[0],
        cross_pair[1],
        stored["probs_two"],
        stored["rounded_two"],
    )
    grad_cq = grad_cq.reshape(length, D)
    grad_pair = jnp.stack([grad_ck, grad_cv]).reshape(2, patch_rows.shape[0], D)
    grad_cross_query = jnp.einsum(
        "nd,ne->de", stored["normed_two"], grad_cq, preferred_element_type=float_type
    )
    grad_cross_pair = jnp.einsum(
        "pd,kpe->kde", patch_rows, grad_pair, preferred_element_type=float_type
    )
    patch_grad = jnp.einsum(
        "kpe,kde->pd", grad_pair, attention[5:7], preferred_element_type=float_type
    )
    grad_normed_two = jnp.einsum(
        "ne,de->nd", grad_cq, attention[4], preferred_element_type=float_type
    )
    grad_from_two, gain_two = norm_backward(
        grad_normed_two, gain_rows[1], stored["unit_two"], stored["rms_two"]
    )
    grad_after_one = grad_after_two + grad_from_two
    branch_one = grad_after_one.astype(brain_type)
    grad_self_out = jnp.einsum(
        "nd,ne->de", stored["mixture_one"], branch_one, preferred_element_type=float_type
    )
    grad_mixture_one = split_heads(
        jnp.einsum("ne,de->nd", branch_one, attention[3], preferred_element_type=float_type).astype(
            brain_type
        )
    )
    heads_in = stored["heads_in"]
    grad_query, grad_key, grad_value = attend_backward(
        grad_mixture_one,
        heads_in[0],
        heads_in[1],
        heads_in[2],
        stored["probs_one"],
        stored["rounded_one"],
    )
    grad_projected = jnp.stack([grad_query, grad_key, grad_value]).reshape(3, length, D)
    grad_self_in = jnp.einsum(
        "nd,kne->kde", stored["normed_one"], grad_projected, preferred_element_type=float_type
    )
    grad_normed_one = jnp.einsum(
        "kne,kde->nd", grad_projected, attention[0:3], preferred_element_type=float_type
    )
    grad_from_one, gain_one = norm_backward(
        grad_normed_one, gain_rows[0], stored["unit_one"], stored["rms_one"]
    )
    hidden_grad = grad_after_one + grad_from_one
    grad_attention = jnp.concatenate(
        [
            grad_self_in,
            grad_self_out[None],
            grad_cross_query[None],
            grad_cross_pair,
            grad_cross_out[None],
        ],
        axis=0,
    )
    grad_gains = jnp.stack([gain_one, gain_two, gain_three])
    return (hidden_grad, patch_grad, (grad_attention, grad_inner, grad_outer, grad_gains))


def fetch_forward(copies):
    widened = (
        lax.all_gather(copies[0], "fsdp", axis=1, tiled=True),
        lax.all_gather(copies[1], "fsdp", axis=1, tiled=True),
        lax.all_gather(copies[2], "fsdp", axis=0, tiled=True),
        lax.all_gather(copies[3], "fsdp", axis=1, tiled=True),
    )
    complete = (
        lax.all_gather(widened[0], "dp", axis=2, tiled=True),
        lax.all_gather(widened[1], "dp", axis=2, tiled=True),
        lax.all_gather(widened[2], "dp", axis=1, tiled=True),
    )
    return (complete[0], complete[1], complete[2], widened[3])


def fetch_backward(copies):
    widened = (
        lax.all_gather(copies[0], "fsdp", axis=1, tiled=True),
        lax.all_gather(copies[1], "fsdp", axis=1, tiled=True),
        lax.all_gather(copies[2], "fsdp", axis=0, tiled=True),
        lax.all_gather(copies[3], "fsdp", axis=1, tiled=True),
    )
    complete = (
        lax.all_gather(widened[0], "dp", axis=2, tiled=True),
        lax.all_gather(widened[1], "dp", axis=2, tiled=True),
        lax.all_gather(widened[2], "dp", axis=1, tiled=True),
    )
    return (complete[0], complete[1], complete[2], widened[3])


def reduce_grads(totals):
    partial_sums = (
        lax.psum_scatter(totals[0], "dp", scatter_dimension=2, tiled=True),
        lax.psum_scatter(totals[1], "dp", scatter_dimension=2, tiled=True),
        lax.psum_scatter(totals[2], "dp", scatter_dimension=1, tiled=True),
    )
    gain_totals = lax.psum(totals[3], "dp")
    return (
        lax.psum_scatter(partial_sums[0], "fsdp", scatter_dimension=1, tiled=True),
        lax.psum_scatter(partial_sums[1], "fsdp", scatter_dimension=1, tiled=True),
        lax.psum_scatter(partial_sums[2], "fsdp", scatter_dimension=0, tiled=True),
        lax.psum_scatter(gain_totals, "fsdp", scatter_dimension=1, tiled=True),
    )


def adam_update(weight, mean_old, square_old, gradient, step_rate, decay_rate):
    mean_new = beta_one * mean_old + (1.0 - beta_one) * gradient
    square_new = beta_two * square_old + (1.0 - beta_two) * gradient * gradient
    corrected = (
        mean_new
        / (1.0 - beta_one**STEP)
        / (jnp.sqrt(square_new / (1.0 - beta_two**STEP)) + adam_epsilon)
    )
    master = weight - step_rate * (corrected + decay_rate * weight)
    return (mean_new, square_new, master, master.astype(jnp.bfloat16))


def on_device(
    hidden_in,
    patches,
    token_segments,
    patch_segments,
    cotangent,
    attention_weights,
    attention_means,
    attention_squares,
    inner_weights,
    inner_means,
    inner_squares,
    outer_weights,
    outer_means,
    outer_squares,
    norm_gains,
    gain_means,
    gain_squares,
):
    copies = (
        attention_weights.astype(brain_type),
        inner_weights.astype(brain_type),
        outer_weights.astype(brain_type),
        norm_gains.astype(brain_type),
    )
    layer_outputs = []
    input_grads = []
    patch_grads = []
    totals = None
    for batch_index in range(hidden_in.shape[0]):
        forward_weights = fetch_forward(copies)
        layer_out, stored = layer_forward(
            forward_weights,
            hidden_in[batch_index, 0],
            patches[batch_index, 0],
            token_segments[batch_index, 0],
            patch_segments[batch_index, 0],
        )
        backward_weights = fetch_backward(copies)
        hidden_grad, patch_grad, gradients = layer_backward(
            backward_weights, stored, cotangent[batch_index, 0], patches[batch_index, 0]
        )
        layer_outputs.append(layer_out)
        input_grads.append(hidden_grad)
        patch_grads.append(patch_grad)
        totals = gradients if totals is None else jax.tree.map(jnp.add, totals, gradients)
    owned_grads = reduce_grads(totals)
    attention_new = adam_update(
        attention_weights,
        attention_means,
        attention_squares,
        owned_grads[0],
        rate_matrix,
        decay_matrix,
    )
    inner_new = adam_update(
        inner_weights, inner_means, inner_squares, owned_grads[1], rate_matrix, decay_matrix
    )
    outer_new = adam_update(
        outer_weights, outer_means, outer_squares, owned_grads[2], rate_matrix, decay_matrix
    )
    gain_new = adam_update(norm_gains, gain_means, gain_squares, owned_grads[3], rate_gain, 0.0)
    hidden_out = jnp.stack(layer_outputs)[:, None]
    hidden_grads = jnp.stack(input_grads)[:, None]
    patch_grads_all = jnp.stack(patch_grads)[:, None]
    return (
        hidden_out,
        hidden_grads,
        patch_grads_all,
        attention_new[0],
        attention_new[1],
        attention_new[2],
        attention_new[3],
        inner_new[0],
        inner_new[1],
        inner_new[2],
        inner_new[3],
        outer_new[0],
        outer_new[1],
        outer_new[2],
        outer_new[3],
        gain_new[0],
        gain_new[1],
        gain_new[2],
        gain_new[3],
    )


def solution(mesh):
    placed = (
        P(None, ("dp", "fsdp"), None, None),
        P(None, ("dp", "fsdp"), None, None),
        P(None, ("dp", "fsdp"), None),
        P(None, ("dp", "fsdp"), None),
        P(None, ("dp", "fsdp"), None, None),
        P(None, "fsdp", "dp"),
        P(None, "fsdp", "dp"),
        P(None, "fsdp", "dp"),
        P(None, "fsdp", "dp"),
        P(None, "fsdp", "dp"),
        P(None, "fsdp", "dp"),
        P("fsdp", "dp"),
        P("fsdp", "dp"),
        P("fsdp", "dp"),
        P(None, "fsdp"),
        P(None, "fsdp"),
        P(None, "fsdp"),
    )
    return jax.shard_map(
        on_device,
        mesh=mesh,
        in_specs=placed,
        out_specs=(
            P(None, ("dp", "fsdp"), None, None),
            P(None, ("dp", "fsdp"), None, None),
            P(None, ("dp", "fsdp"), None, None),
            P(None, "fsdp", "dp"),
            P(None, "fsdp", "dp"),
            P(None, "fsdp", "dp"),
            P(None, "fsdp", "dp"),
            P(None, "fsdp", "dp"),
            P(None, "fsdp", "dp"),
            P(None, "fsdp", "dp"),
            P(None, "fsdp", "dp"),
            P("fsdp", "dp"),
            P("fsdp", "dp"),
            P("fsdp", "dp"),
            P("fsdp", "dp"),
            P(None, "fsdp"),
            P(None, "fsdp"),
            P(None, "fsdp"),
            P(None, "fsdp"),
        ),
        check_vma=False,
    )
```

profile of v0, /device:TPU:0, one launch (start us, length us, event | category | flops | bytes accessed | tf_op | source)
XLA Modules:
  0.0 1277.1 jit_solution(9727439426056397318)
XLA Ops:
  9.8 22.8 %all-gather.6.cloned.1.call-done = bf16[8,768,96]{2,0,1:T(8,128)(2,1)} async-done(((bf16[8,192,96]{2,0,1:T(8,128)(2,1)}), bf16[8,768,96]{2,0,1:T(8,128)(2,1)}) %all-gather.6.cloned.1.call-update) | async-done | bytes 1179664 | tf_op jit(solution)/shard_map/all_gather | solution.py:257
  35.8 9.0 all_gather.17
  54.9 118.2 %all-gather.8.cloned.1.call-done = bf16[8,768,768]{1,0,2:T(8,128)(2,1)} async-done(((bf16[8,768,96]{1,0,2:T(8,128)(2,1)}), bf16[8,768,768]{1,0,2:T(8,128)(2,1)}) %all-gather.8.cloned.1.call-update) | async-done | bytes 9437200 | tf_op jit(solution)/shard_map/all_gather | solution.py:263
  173.2 7.1 slice.179
  180.2 8.3 copy.479
  188.5 18.3 %fusion.261 = (bf16[1,768,768]{1,0,2:T(2,128)(2,1)}, bf16[1,768,768]{1,0,2:T(2,128)(2,1)}, bf16[1,768,768]{1,0,2:T(2,128)(2,1)}) fusion(bf16[8,768,768]{1,0,2:T(8,128)(2,1)} %all-gather.8.cloned.1.call-done), kind=kLoop, calls=%fused_computation.380 | loop fusion | bytes 7077888 | tf_op jit(solution)/shard_map/slice | solution.py:119
  265.6 14.4 %fusion.271 = (f32[12,256]{1,0:T(8,128)S(1)}, f32[12,256,2048]{2,1,0:T(8,128)}) fusion(pred[256,2048]{1,0:T(8,128)(4,1)} %broadcast_compare_fusion.1, bf16[256,12,64]{0,2,1:T(8,128)(2,1)S(1)} %bitcast.442, bf16[2048,12,64]{0,2,1:T(8,128)(2,1)} %bitcast.427), kind=kOutput, calls=%fused_computation.390 | convolution fusion | flops 830474240 | bytes 29241344 | tf_op jit(solution)/shard_map/sub | solution.py:51
  287.0 11.6 fusion.101
  300.7 7.4 convert_bitcast_fusion
  311.3 14.4 %fusion.269 = (f32[12,256]{1,0:T(8,128)S(1)}, f32[12,256,2048]{2,1,0:T(8,128)}) fusion(pred[256,2048]{1,0:T(8,128)(4,1)} %broadcast_compare_fusion, bf16[256,12,64]{0,2,1:T(8,128)(2,1)S(1)} %bitcast.444, bf16[2048,12,64]{0,2,1:T(8,128)(2,1)} %bitcast.429), kind=kOutput, calls=%fused_computation.388 | convolution fusion | flops 830474240 | bytes 29241344 | tf_op jit(solution)/shard_map/sub | solution.py:51
  325.8 11.5 fusion.104
  355.5 116.4 %reduce-scatter.15.cloned.1.call-done = f32[2048,96]{0,1:T(8,128)} async-done(((f32[2048,768]{0,1:T(8,128)}), f32[2048,96]{0,1:T(8,128)}) %reduce-scatter.15.cloned.1.call-update) | async-done | bytes 786448 | tf_op jit(solution)/shard_map/reduce_scatter | solution.py:289
  471.9 24.8 %reduce-scatter.17.cloned.1.call-done = f32[512,96]{0,1:T(8,128)} async-done(((f32[2048,96]{0,1:T(8,128)}), f32[512,96]{0,1:T(8,128)}) %reduce-scatter.17.cloned.1.call-update) | async-done | bytes 196624 | tf_op jit(solution)/shard_map/reduce_scatter | solution.py:295
  505.6 60.4 %all-gather.12.cloned.1.call-done = bf16[2048,768]{0,1:T(8,128)(2,1)} async-done(((bf16[2048,96]{0,1:T(8,128)(2,1)}), bf16[2048,768]{0,1:T(8,128)(2,1)}) %all-gather.12.cloned.1.call-update) | async-done | bytes 3145744 | tf_op jit(solution)/shard_map/all_gather | solution.py:265
  571.9 7.8 fusion.89
  591.4 11.2 fusion.29
  602.6 18.0 %multiply_reduce_fusion = (f32[12,256]{1,0:T(8,128)}, f32[12,256,2048]{2,1,0:T(8,128)}) fusion(f32[12,256,2048]{2,1,0:T(8,128)} %get-tuple-element.202, f32[12,256]{1,0:T(8,128)} %copy-done.110, bf16[256,12,64]{0,2,1:T(8,128)(2,1)} %bitcast.478, bf16[2048,12,64]{0,2,1:T(8,128)(2,1)} %bitcast.441), kind=kOutput, calls=%fused_computation.5 | convolution fusion | flops 824177664 | bytes 53895168 | tf_op jit(solution)/shard_map/qhe,khe->hqk/dot_general | solution.py:68
  621.4 11.8 add_bitcast_fusion
  633.9 12.0 fusion.26
  653.6 16.7 %multiply_convert_fusion = bf16[12,256,2048]{2,1,0:T(8,128)(2,1)S(1)} fusion(f32[12,256,2048]{2,1,0:T(8,128)} %get-tuple-element.215, f32[12,256]{1,0:T(8,128)} %get-tuple-element.214, f32[12,256,2048]{2,1,0:T(8,128)} %get-tuple-element.202, f32[12,256]{1,0:T(8,128)} %copy-done.110), kind=kLoop, calls=%fused_computation.4 | loop fusion | flops 25165824 | bytes 62939136 | tf_op jit(solution)/shard_map/convert_element_type | solution.py:75
  677.7 17.6 %multiply_reduce_fusion.1 = (f32[12,256]{1,0:T(8,128)S(1)}, f32[12,256,2048]{2,1,0:T(8,128)}) fusion(f32[12,256,2048]{2,1,0:T(8,128)} %get-tuple-element.208, f32[12,256]{1,0:T(8,128)S(1)} %copy-done.109, bf16[256,12,64]{0,2,1:T(8,128)(2,1)S(1)} %bitcast.472, bf16[2048,12,64]{0,2,1:T(8,128)(2,1)} %bitcast.439), kind=kOutput, calls=%fused_computation.7 | convolution fusion | flops 824177664 | bytes 53895168 | tf_op jit(solution)/shard_map/qhe,khe->hqk/dot_general | solution.py:68
  695.3 16.5 %multiply_convert_fusion.1 = bf16[12,256,2048]{2,1,0:T(8,128)(2,1)S(1)} fusion(f32[12,256,2048]{2,1,0:T(8,128)} %get-tuple-element.217, f32[12,256]{1,0:T(8,128)S(1)} %get-tuple-element.216, f32[12,256,2048]{2,1,0:T(8,128)} %get-tuple-element.208, f32[12,256]{1,0:T(8,128)S(1)} %copy-done.109), kind=kLoop, calls=%fused_computation.6 | loop fusion | flops 25165824 | bytes 62939136 | tf_op jit(solution)/shard_map/convert_element_type | solution.py:75
  719.9 9.8 fusion.99
  731.7 8.8 fusion.100
  784.2 7.4 bitcast_dynamic-update-slice_fusion.2
  801.4 8.9 bitcast_dynamic-update-slice_fusion.3
  812.3 13.1 %add.227 = f32[8,768,768]{1,2,0:T(8,128)} add(f32[8,768,768]{1,2,0:T(8,128)} %bitcast_dynamic-update-slice_fusion.7, f32[8,768,768]{1,2,0:T(8,128)S(1)} %bitcast_dynamic-update-slice_fusion.4) | non-fusion elementwise | flops 4718592 | bytes 56623104 | tf_op jit(solution)/shard_map/add | solution.py:357
  855.0 299.2 %reduce-scatter.11.cloned.1.call-done = f32[8,768,96]{1,2,0:T(8,128)} async-done(((f32[8,768,768]{1,2,0:T(8,128)}), f32[8,768,96]{1,2,0:T(8,128)}) %reduce-scatter.11.cloned.1.call-update) | async-done | bytes 2359312 | tf_op jit(solution)/shard_map/reduce_scatter | solution.py:287
  1184.6 9.1 maximum_bitcast_fusion
  1194.7 19.9 %psum.8 = f32[3,192]{1,0:T(4,128)S(1)} all-reduce(f32[3,192]{1,0:T(4,128)S(1)} %copy.478), channel_id=1, replica_groups=mesh['dp'=8,'fsdp'=4] {'dp'}, use_global_device_ids=true, to_apply=%region_36.37 | all-reduce | flops 576 | bytes 4608 | tf_op jit(solution)/shard_map/psum | solution.py:291
  1215.2 7.1 all-reduce.3.cloned.1.call-done
  1226.0 31.7 %reduce-scatter.19.cloned.1.call-done = f32[192,768]{1,0:T(8,128)} async-done(((f32[768,768]{1,0:T(8,128)}), f32[192,768]{1,0:T(8,128)}) %reduce-scatter.19.cloned.1.call-update) | async-done | bytes 589840
  (441 shorter events, 289.1 us)
Async XLA Ops:
  7.2 25.3 %all-gather.6.cloned.1.call-start = ((), (), s32[]{:S(2)}) async-start(), calls=%async_computation.6 | async-start | bytes 1966080 | tf_op jit(solution)/shard_map/all_gather | solution.py:257
  9.7 35.3 %copy-start.111 = (f32[3,192]{1,0:T(4,128)S(1)}, f32[3,192]{1,0:T(4,128)}, u32[]{:S(2)}) copy-start(f32[3,192]{1,0:T(4,128)} %param.31) | copy-start | bytes 6916
  9.7 35.3 %copy-start.127 = (s32[2,1,256]{2,1,0:T(1,128)S(1)}, s32[2,1,256]{2,1,0:T(1,128)}, u32[]{:S(2)}) copy-start(s32[2,1,256]{2,1,0:T(1,128)} %param.19) | copy-start | bytes 6148
  9.7 35.3 %copy-start.47 = (bf16[2,1,256,768]{3,2,1,0:T(8,128)(2,1)S(1)}, bf16[2,1,256,768]{3,2,1,0:T(8,128)(2,1)}, u32[]{:S(2)}) copy-start(bf16[2,1,256,768]{3,2,1,0:T(8,128)(2,1)} %param.17) | copy-start | bytes 2359300
  9.7 41.4 %copy-start.113 = (s32[2,1,2048]{2,1,0:T(1,128)S(1)}, s32[2,1,2048]{2,1,0:T(1,128)}, u32[]{:S(2)}) copy-start(s32[2,1,2048]{2,1,0:T(1,128)} %param.20) | copy-start | bytes 49156
  9.7 163.5 %all-gather.8.cloned.1.call-start = ((), (), s32[]{:S(2)}) async-start(), calls=%async_computation.7 | async-start | bytes 10616832 | tf_op jit(solution)/shard_map/all_gather | solution.py:263
  35.8 302.3 %all-gather.10.cloned.1.call-start = ((), (), s32[]{:S(2)}) async-start(), calls=%async_computation.8 | async-start | bytes 7077888 | tf_op jit(solution)/shard_map/all_gather | solution.py:264
  44.9 427.0 %reduce-scatter.15.cloned.1.call-start = ((), (), s32[]{:S(2)}) async-start(), calls=%async_computation.12 | async-start | bytes 7077888 | tf_op jit(solution)/shard_map/reduce_scatter | solution.py:289
  51.1 175.6 %copy-start.115 = (f32[768]{0:T(1024)}, f32[768]{0:T(1024)S(1)}, u32[]{:S(2)}) copy-start(f32[768]{0:T(1024)S(1)} %get-tuple-element.151) | copy-start | bytes 9220
  51.1 228.9 %copy-start.99 = (f32[768]{0:T(1024)}, f32[768]{0:T(1024)S(1)}, u32[]{:S(2)}) copy-start(f32[768]{0:T(1024)S(1)} %get-tuple-element.150) | copy-start | bytes 9220
  54.9 163.0 %copy-start.121 = (f32[256]{0:T(256)}, f32[256]{0:T(256)S(1)}, u32[]{:S(2)}) copy-start(f32[256]{0:T(256)S(1)} %get-tuple-element.225) | copy-start | bytes 3076
  54.9 171.8 %copy-start.123 = (f32[256]{0:T(256)}, f32[256]{0:T(256)S(1)}, u32[]{:S(2)}) copy-start(f32[256]{0:T(256)S(1)} %get-tuple-element.226) | copy-start | bytes 3076
  217.9 62.2 %copy-start.4 = (bf16[1,768,768]{2,1,0:T(8,128)(2,1)}, bf16[1,768,768]{2,1,0:T(8,128)(2,1)S(1)}, u32[]{:S(2)}) copy-start(bf16[1,768,768]{2,1,0:T(8,128)(2,1)S(1)} %copy.482) | copy-start | bytes 3538948
  241.7 56.9 %copy-start.8 = (f32[256,768]{1,0:T(8,128)}, f32[256,768]{1,0:T(8,128)S(1)}, u32[]{:S(2)}) copy-start(f32[256,768]{1,0:T(8,128)S(1)} %get-tuple-element.206) | copy-start | bytes 2359300
  249.7 87.6 %copy-start.10 = (f32[256,768]{1,0:T(8,128)}, f32[256,768]{1,0:T(8,128)S(1)}, u32[]{:S(2)}) copy-start(f32[256,768]{1,0:T(8,128)S(1)} %get-tuple-element.200) | copy-start | bytes 2359300
  249.8 30.2 %copy-start.103 = (f32[256]{0:T(256)}, f32[256]{0:T(256)S(1)}, u32[]{:S(2)}) copy-start(f32[256]{0:T(256)S(1)} %add_rsqrt_fusion.1) | copy-start | bytes 3076
  299.2 289.5 %copy-start.12 = (f32[256,768]{1,0:T(8,128)}, f32[256,768]{1,0:T(8,128)S(1)}, u32[]{:S(2)}) copy-start(f32[256,768]{1,0:T(8,128)S(1)} %get-tuple-element.210) | copy-start | bytes 2359300
  338.1 283.3 %copy-start.14 = (f32[256,768]{1,0:T(8,128)}, f32[256,768]{1,0:T(8,128)S(1)}, u32[]{:S(2)}) copy-start(f32[256,768]{1,0:T(8,128)S(1)} %get-tuple-element.212) | copy-start | bytes 2359300
  355.5 141.3 %reduce-scatter.17.cloned.1.call-start = ((), (), s32[]{:S(2)}) async-start(), calls=%async_computation.13 | async-start | bytes 983040 | tf_op jit(solution)/shard_map/reduce_scatter | solution.py:295
  471.9 94.1 %all-gather.12.cloned.1.call-start = ((), (), s32[]{:S(2)}) async-start(), calls=%async_computation.9 | async-start | bytes 3538944 | tf_op jit(solution)/shard_map/all_gather | solution.py:265
  505.5 333.9 %reduce-scatter.13.cloned.1.call-start = ((), (), s32[]{:S(2)}) async-start(), calls=%async_computation.11 | async-start | bytes 14155776 | tf_op jit(solution)/shard_map/reduce_scatter | solution.py:288
  633.2 521.0 %reduce-scatter.11.cloned.1.call-start = ((), (), s32[]{:S(2)}) async-start(), calls=%async_computation.10 | async-start | bytes 21233664 | tf_op jit(solution)/shard_map/reduce_scatter | solution.py:287
  825.4 368.3 %reduce-scatter.21.cloned.1.call-start = ((), (), s32[]{:S(2)}) async-start(), calls=%async_computation.15 | async-start | bytes 491520
  833.6 388.7 %all-reduce.3.cloned.1.call-start = ((), (), s32[]{:S(2)}) async-start(), calls=%async_computation.16 | async-start | bytes 3145728
  843.1 414.7 %reduce-scatter.19.cloned.1.call-start = ((), (), s32[]{:S(2)}) async-start(), calls=%async_computation.14 | async-start | bytes 2949120
  1184.6 30.0 %copy-start.112 = (f32[3,192]{1,0:T(4,128)S(1)}, f32[3,192]{1,0:T(4,128)}, u32[]{:S(2)}) copy-start(f32[3,192]{1,0:T(4,128)} %param.31) | copy-start | bytes 6916
  1184.6 30.0 %copy-start.117 = (f32[3,192]{1,0:T(4,128)S(1)}, f32[3,192]{1,0:T(4,128)}, u32[]{:S(2)}) copy-start(f32[3,192]{1,0:T(4,128)} %param.33) | copy-start | bytes 6916
  1184.6 30.0 %copy-start.118 = (f32[3,192]{1,0:T(4,128)S(1)}, f32[3,192]{1,0:T(4,128)}, u32[]{:S(2)}) copy-start(f32[3,192]{1,0:T(4,128)} %param.32) | copy-start | bytes 6916
  1184.6 38.9 %copy-start.76 = (f32[2,192,256]{2,1,0:T(8,128)S(1)}, f32[2,192,256]{2,1,0:T(8,128)}, u32[]{:S(2)}) copy-start(f32[2,192,256]{2,1,0:T(8,128)} %param.25) | copy-start | bytes 1179652
  1223.5 37.0 %copy-start.52 = (f32[8,192,96]{1,2,0:T(8,128)S(1)}, f32[8,192,96]{1,2,0:T(8,128)}, u32[]{:S(2)}) copy-start(f32[8,192,96]{1,2,0:T(8,128)} %copy.439) | copy-start | bytes 1769476
  1223.5 37.0 %copy-start.53 = (f32[8,192,96]{1,2,0:T(8,128)S(1)}, f32[8,192,96]{1,2,0:T(8,128)}, u32[]{:S(2)}) copy-start(f32[8,192,96]{1,2,0:T(8,128)} %copy.426) | copy-start | bytes 1769476
  1223.5 37.0 %copy-start.54 = (f32[8,192,96]{1,2,0:T(8,128)S(1)}, f32[8,192,96]{1,2,0:T(8,128)}, u32[]{:S(2)}) copy-start(f32[8,192,96]{1,2,0:T(8,128)} %copy.437) | copy-start | bytes 1769476
  (115 other events, 627.1 us)
Sparse Core Ops, SparseCore 0:
  10.1 22.3 all-gather.5
  35.9 137.2 all-gather.7
  175.2 97.6 all-gather.9
  355.6 116.2 reduce-scatter.14
  474.2 22.4 reduce-scatter.16
  505.7 60.2 all-gather.11
  633.3 206.0 reduce-scatter.12
  843.3 310.8 reduce-scatter.10
  1157.3 19.8 reduce-scatter.20
  1179.4 42.8 all-reduce.2
  1224.9 32.8 reduce-scatter.18
where the time goes:
time: 1280 us
  waiting for transfers between devices  686 us (54%)
  matrix products  296 us (23%)
  local copies, waits for them, and re-layouts  161 us (13%)
  other arithmetic  75.5 us (6%)
  blocking collectives  40.7 us (3%)
  between operations  16.7 us (1%)
    reduce_scatter x1, waiting for transfers between devices, reduce_grads(): lax.psum_scatter(totals[0], 'dp', scatter_dimension=2, tiled=True)  299 us
    all_gather x1, waiting for transfers between devices, fetch_forward(): lax.all_gather(widened[0], 'dp', axis=2, tiled=True)  118 us
    reduce_scatter x1, waiting for transfers between devices, reduce_grads(): lax.psum_scatter(totals[2], 'dp', scatter_dimension=1, tiled=True)  116 us
    unnamed x293, local copies, waits for them, and re-layouts  80.4 us
    all_gather x1, waiting for transfers between devices, fetch_forward(): lax.all_gather(widened[2], 'dp', axis=1, tiled=True)  60.4 us
    dot_general x4, matrix products, attend_backward(): jnp.einsum('qhe,khe->hqk', grad_mixture, value_heads, preferred_element_t...  41.4 us
    unnamed x14, waiting for transfers between devices  39 us
    sub x4, matrix products, softmax_rows(): raised = jnp.exp(scores - row_maximum)  37.1 us
  transfers between devices with their start and end apart: 11, of which 9 were waited for; matrix products, arithmetic and copies ran while one was open for 32% of the time, Pallas kernels for 0%

commit v1 on v0

--- a/solution.py
+++ b/solution.py
@@ -254,7 +254,9 @@
 
 def fetch_forward(copies):
     widened = (
-        lax.all_gather(copies[0], "fsdp", axis=1, tiled=True),
+        jnp.concatenate(
+            lax.all_to_all(jnp.stack([copies[0]] * lax.axis_size("fsdp")), "fsdp", 0, 0), axis=1
+        ),
         lax.all_gather(copies[1], "fsdp", axis=1, tiled=True),
         lax.all_gather(copies[2], "fsdp", axis=0, tiled=True),
         lax.all_gather(copies[3], "fsdp", axis=1, tiled=True),

time: 1280 us -> 1350 us (1.055)
  local copies, waits for them, and re-layouts: 161 us -> 232 us
  waiting for transfers between devices: 686 us -> 660 us
  blocking collectives: 40.7 us -> 63.2 us
    all_gather x1 -> x2, waiting for transfers between devices: 22.8 us -> 109 us  [the longest x1 109 us: fetch_backward(): lax.all_gather(widened[0], 'dp', axis=2, tiled=True)]
    unnamed x14 -> x15, waiting for transfers between devices: 39 us -> 0.71 us
    all_gather x1, waiting for transfers between devices: 60.4 us -> 22.2 us  [fetch_forward(): lax.all_gather(widened[2], 'dp', axis=1, tiled=True)]
    slice x0 -> x3, local copies, waits for them, and re-layouts: none -> 33.5 us  [the longest x1 18.7 us: layer_backward(): attention[3]]
    unnamed x293 -> x306, local copies, waits for them, and re-layouts: 80.4 us -> 113 us
    reduce_scatter x1, waiting for transfers between devices: 299 us -> 274 us  [reduce_grads(): lax.psum_scatter(totals[0], 'dp', scatter_dimension=2, tiled=True)]
    all_to_all x0 -> x1, blocking collectives: none -> 24.1 us  [fetch_forward(): lax.all_to_all(jnp.stack([copies[0]] * lax.axis_size('fsdp')), 'fsdp', 0, 0)]
  transfers between devices with their start and end apart: 11 -> 12, of which waited for: 9 -> 6; matrix products, arithmetic and copies ran while one was open for 32% -> 36% of each run, Pallas kernels for 0% -> 0%
where the time goes in v1:
time: 1350 us
  waiting for transfers between devices  660 us (49%)
  matrix products  298 us (22%)
  local copies, waits for them, and re-layouts  232 us (17%)
  other arithmetic  74.7 us (6%)
  blocking collectives  63.2 us (5%)
  between operations  18.1 us (1%)
    reduce_scatter x1, waiting for transfers between devices, reduce_grads(): lax.psum_scatter(totals[0], 'dp', scatter_dimension=2, tiled=True)  274 us
    all_gather x1, waiting for transfers between devices, fetch_forward(): lax.all_gather(widened[0], 'dp', axis=2, tiled=True)  119 us
    reduce_scatter x1, waiting for transfers between devices, reduce_grads(): lax.psum_scatter(totals[2], 'dp', scatter_dimension=1, tiled=True)  116 us
    unnamed x306, local copies, waits for them, and re-layouts  113 us
    all_gather x1, waiting for transfers between devices, fetch_backward(): lax.all_gather(widened[0], 'dp', axis=2, tiled=True)  109 us
    dot_general x4, matrix products, attend_backward(): jnp.einsum('qhe,khe->hqk', grad_mixture, value_heads, preferred_element_t...  41 us
    sub x4, matrix products, softmax_rows(): raised = jnp.exp(scores - row_maximum)  38 us
    convert_element_type x4, other arithmetic, attend_backward(): grad_scores = (probabilities * (grad_probs - row_inner)).astype(brain_type)  34.4 us
  transfers between devices with their start and end apart: 12, of which 6 were waited for; matrix products, arithmetic and copies ran while one was open for 36% of the time, Pallas kernels for 0%

profile of v1, /device:TPU:0, one launch (start us, length us, event | category | flops | bytes accessed | tf_op | source)
XLA Modules:
  0.0 1346.0 jit_solution(9650435375077015629)
XLA Ops:
  10.8 24.1 %all_to_all.6 = bf16[4,8,192,96]{3,2,1,0:T(8,128)(2,1)S(1)} all-to-all(bf16[4,8,192,96]{3,2,1,0:T(8,128)(2,1)S(1)} %stack.129), channel_id=1, replica_groups=mesh['dp'=8,'fsdp'=4] {'fsdp'}, dimensions={0} | all-to-all | bytes 2359296 | tf_op jit(solution)/shard_map/all_to_all | solution.py:258
  38.8 8.3 all_gather.18
  57.2 119.3 %all-gather.7.cloned.1.call-done = bf16[8,768,768]{1,0,2:T(8,128)(2,1)} async-done(((bf16[8,768,96]{1,0,2:T(8,128)(2,1)}), bf16[8,768,768]{1,0,2:T(8,128)(2,1)}) %all-gather.7.cloned.1.call-update) | async-done | bytes 9437200 | tf_op jit(solution)/shard_map/all_gather | solution.py:265
  183.6 8.1 copy.498
  191.7 17.7 %fusion.260 = (bf16[1,768,768]{1,0,2:T(2,128)(2,1)}, bf16[1,768,768]{1,0,2:T(2,128)(2,1)S(1)}, bf16[1,768,768]{1,0,2:T(2,128)(2,1)}) fusion(bf16[8,768,768]{1,0,2:T(8,128)(2,1)} %all-gather.7.cloned.1.call-done), kind=kLoop, calls=%fused_computation.379 | loop fusion | bytes 7077888 | tf_op jit(solution)/shard_map/slice | solution.py:119
  268.8 15.1 %fusion.270 = (f32[12,256]{1,0:T(8,128)}, f32[12,256,2048]{2,1,0:T(8,128)}) fusion(pred[256,2048]{1,0:T(8,128)(4,1)} %broadcast_compare_fusion.1, bf16[256,12,64]{0,2,1:T(8,128)(2,1)S(1)} %bitcast.451, bf16[2048,12,64]{0,2,1:T(8,128)(2,1)} %bitcast.435), kind=kOutput, calls=%fused_computation.389 | convolution fusion | flops 830474240 | bytes 29241344 | tf_op jit(solution)/shard_map/sub | solution.py:51
  291.5 11.5 fusion.99
  315.7 14.4 %fusion.268 = (f32[12,256]{1,0:T(8,128)S(1)}, f32[12,256,2048]{2,1,0:T(8,128)}) fusion(pred[256,2048]{1,0:T(8,128)(4,1)} %broadcast_compare_fusion, bf16[256,12,64]{0,2,1:T(8,128)(2,1)S(1)} %bitcast.453, bf16[2048,12,64]{0,2,1:T(8,128)(2,1)} %bitcast.437), kind=kOutput, calls=%fused_computation.387 | convolution fusion | flops 830474240 | bytes 29241344 | tf_op jit(solution)/shard_map/sub | solution.py:51
  330.2 11.5 fusion.102
  360.3 115.6 %reduce-scatter.15.cloned.1.call-done = f32[2048,96]{0,1:T(8,128)} async-done(((f32[2048,768]{0,1:T(8,128)}), f32[2048,96]{0,1:T(8,128)}) %reduce-scatter.15.cloned.1.call-update) | async-done | bytes 786448 | tf_op jit(solution)/shard_map/reduce_scatter | solution.py:291
  479.3 19.2 %reduce-scatter.17.cloned.1.call-done = f32[512,96]{0,1:T(8,128)} async-done(((f32[2048,96]{0,1:T(8,128)}), f32[512,96]{0,1:T(8,128)}) %reduce-scatter.17.cloned.1.call-update) | async-done | bytes 196624 | tf_op jit(solution)/shard_map/reduce_scatter | solution.py:297
  507.0 108.9 %all-gather.15.cloned.1.call-done = bf16[8,768,768]{1,0,2:T(8,128)(2,1)} async-done(((bf16[8,768,96]{1,0,2:T(8,128)(2,1)}), bf16[8,768,768]{1,0,2:T(8,128)(2,1)}) %all-gather.15.cloned.1.call-update) | async-done | bytes 9437200 | tf_op jit(solution)/shard_map/all_gather | solution.py:280
  615.9 18.7 %fusion.259 = (bf16[1,768,768]{1,0,2:T(2,128)(2,1)}, bf16[1,768,768]{1,0,2:T(2,128)(2,1)}, bf16[1,768,768]{1,0,2:T(2,128)(2,1)}) fusion(bf16[8,768,768]{1,0,2:T(8,128)(2,1)} %all-gather.15.cloned.1.call-done), kind=kLoop, calls=%fused_computation.378 | loop fusion | bytes 7077888 | tf_op jit(solution)/shard_map/slice | solution.py:217
  653.9 22.2 %all-gather.11.cloned.1.call-done = bf16[2048,768]{0,1:T(8,128)(2,1)} async-done(((bf16[2048,96]{0,1:T(8,128)(2,1)}), bf16[2048,768]{0,1:T(8,128)(2,1)}) %all-gather.11.cloned.1.call-update) | async-done | bytes 3145744 | tf_op jit(solution)/shard_map/all_gather | solution.py:267
  681.7 7.8 fusion.87
  700.4 11.4 fusion.29
  711.8 17.6 %multiply_reduce_fusion = (f32[12,256]{1,0:T(8,128)}, f32[12,256,2048]{2,1,0:T(8,128)}) fusion(f32[12,256,2048]{2,1,0:T(8,128)} %get-tuple-element.205, f32[12,256]{1,0:T(8,128)S(1)} %copy-done.114, bf16[256,12,64]{0,2,1:T(8,128)(2,1)S(1)} %bitcast.487, bf16[2048,12,64]{0,2,1:T(8,128)(2,1)} %bitcast.450), kind=kOutput, calls=%fused_computation.5 | convolution fusion | flops 824177664 | bytes 53895168 | tf_op jit(solution)/shard_map/qhe,khe->hqk/dot_general | solution.py:68
  731.4 11.5 add_bitcast_fusion
  743.6 12.0 fusion.26
  763.3 16.7 %multiply_convert_fusion = bf16[12,256,2048]{2,1,0:T(8,128)(2,1)S(1)} fusion(f32[12,256,2048]{2,1,0:T(8,128)} %get-tuple-element.218, f32[12,256]{1,0:T(8,128)} %get-tuple-element.217, f32[12,256,2048]{2,1,0:T(8,128)} %get-tuple-element.205, f32[12,256]{1,0:T(8,128)} %copy-done.113), kind=kLoop, calls=%fused_computation.4 | loop fusion | flops 25165824 | bytes 62939136 | tf_op jit(solution)/shard_map/convert_element_type | solution.py:75
  787.4 17.6 %multiply_reduce_fusion.1 = (f32[12,256]{1,0:T(8,128)S(1)}, f32[12,256,2048]{2,1,0:T(8,128)}) fusion(f32[12,256,2048]{2,1,0:T(8,128)} %get-tuple-element.211, f32[12,256]{1,0:T(8,128)S(1)} %copy-done.112, bf16[256,12,64]{0,2,1:T(8,128)(2,1)S(1)} %bitcast.481, bf16[2048,12,64]{0,2,1:T(8,128)(2,1)} %bitcast.448), kind=kOutput, calls=%fused_computation.7 | convolution fusion | flops 824177664 | bytes 53895168 | tf_op jit(solution)/shard_map/qhe,khe->hqk/dot_general | solution.py:68
  805.0 16.5 %multiply_convert_fusion.1 = bf16[12,256,2048]{2,1,0:T(8,128)(2,1)S(1)} fusion(f32[12,256,2048]{2,1,0:T(8,128)} %get-tuple-element.220, f32[12,256]{1,0:T(8,128)S(1)} %get-tuple-element.219, f32[12,256,2048]{2,1,0:T(8,128)} %get-tuple-element.211, f32[12,256]{1,0:T(8,128)S(1)} %copy-done.112), kind=kLoop, calls=%fused_computation.6 | loop fusion | flops 25165824 | bytes 62939136 | tf_op jit(solution)/shard_map/convert_element_type | solution.py:75
  829.6 9.8 fusion.97
  841.4 8.8 fusion.98
  893.9 7.4 bitcast_dynamic-update-slice_fusion.2
  911.2 8.9 bitcast_dynamic-update-slice_fusion.3
  922.0 13.0 add.227
  942.3 8.1 copy.506
  968.7 7.6 slice.219
  988.2 273.6 %reduce-scatter.11.cloned.1.call-done = f32[8,768,96]{1,2,0:T(8,128)} async-done(((f32[8,768,768]{1,2,0:T(8,128)}), f32[8,768,96]{1,2,0:T(8,128)}) %reduce-scatter.11.cloned.1.call-update) | async-done | bytes 2359312 | tf_op jit(solution)/shard_map/reduce_scatter | solution.py:289
  1292.3 9.5 maximum_bitcast_fusion
  1302.7 19.1 %psum.8 = f32[3,192]{1,0:T(4,128)S(1)} all-reduce(f32[3,192]{1,0:T(4,128)S(1)} %copy.496), channel_id=1, replica_groups=mesh['dp'=8,'fsdp'=4] {'dp'}, use_global_device_ids=true, to_apply=%region_36.37 | all-reduce | flops 576 | bytes 4608 | tf_op jit(solution)/shard_map/psum | solution.py:293
  (465 shorter events, 336.4 us)
Async XLA Ops:
  8.0 168.5 %all-gather.7.cloned.1.call-start = ((), (), s32[]{:S(2)}) async-start(), calls=%async_computation.7 | async-start | bytes 10616832 | tf_op jit(solution)/shard_map/all_gather | solution.py:265
  36.5 16.9 %copy-start.117 = (s32[2,1,2048]{2,1,0:T(1,128)S(1)}, s32[2,1,2048]{2,1,0:T(1,128)}, u32[]{:S(2)}) copy-start(s32[2,1,2048]{2,1,0:T(1,128)} %param.20) | copy-start | bytes 49156
  38.8 303.7 %all-gather.9.cloned.1.call-start = ((), (), s32[]{:S(2)}) async-start(), calls=%async_computation.8 | async-start | bytes 7077888 | tf_op jit(solution)/shard_map/all_gather | solution.py:266
  47.1 428.7 %reduce-scatter.15.cloned.1.call-start = ((), (), s32[]{:S(2)}) async-start(), calls=%async_computation.14 | async-start | bytes 7077888 | tf_op jit(solution)/shard_map/reduce_scatter | solution.py:291
  53.4 170.6 %copy-start.119 = (f32[768]{0:T(1024)}, f32[768]{0:T(1024)S(1)}, u32[]{:S(2)}) copy-start(f32[768]{0:T(1024)S(1)} %get-tuple-element.151) | copy-start | bytes 9220
  53.4 230.4 %copy-start.100 = (f32[768]{0:T(1024)}, f32[768]{0:T(1024)S(1)}, u32[]{:S(2)}) copy-start(f32[768]{0:T(1024)S(1)} %get-tuple-element.150) | copy-start | bytes 9220
  57.2 162.3 %copy-start.125 = (f32[256]{0:T(256)}, f32[256]{0:T(256)S(1)}, u32[]{:S(2)}) copy-start(f32[256]{0:T(256)S(1)} %get-tuple-element.228) | copy-start | bytes 3076
  57.2 166.8 %copy-start.127 = (f32[256]{0:T(256)}, f32[256]{0:T(256)S(1)}, u32[]{:S(2)}) copy-start(f32[256]{0:T(256)S(1)} %get-tuple-element.229) | copy-start | bytes 3076
  228.7 16.7 %copy-start.64 = (bf16[1,256,768]{1,2,0:T(8,128)(2,1)}, bf16[1,256,768]{1,2,0:T(8,128)(2,1)S(1)}, u32[]{:S(2)}) copy-start(bf16[1,256,768]{1,2,0:T(8,128)(2,1)S(1)} %copy.416) | copy-start | bytes 1179652
  241.6 61.4 %copy-start.6 = (f32[256,768]{1,0:T(8,128)}, f32[256,768]{1,0:T(8,128)S(1)}, u32[]{:S(2)}) copy-start(f32[256,768]{1,0:T(8,128)S(1)} %get-tuple-element.209) | copy-start | bytes 2359300
  252.8 88.9 %copy-start.8 = (f32[256,768]{1,0:T(8,128)}, f32[256,768]{1,0:T(8,128)S(1)}, u32[]{:S(2)}) copy-start(f32[256,768]{1,0:T(8,128)S(1)} %get-tuple-element.203) | copy-start | bytes 2359300
  253.0 30.9 %copy-start.107 = (f32[256]{0:T(256)}, f32[256]{0:T(256)S(1)}, u32[]{:S(2)}) copy-start(f32[256]{0:T(256)S(1)} %add_rsqrt_fusion.1) | copy-start | bytes 3076
  303.7 394.8 %copy-start.10 = (f32[256,768]{1,0:T(8,128)}, f32[256,768]{1,0:T(8,128)S(1)}, u32[]{:S(2)}) copy-start(f32[256,768]{1,0:T(8,128)S(1)} %get-tuple-element.213) | copy-start | bytes 2359300
  342.4 388.9 %copy-start.12 = (f32[256,768]{1,0:T(8,128)}, f32[256,768]{1,0:T(8,128)S(1)}, u32[]{:S(2)}) copy-start(f32[256,768]{1,0:T(8,128)S(1)} %get-tuple-element.215) | copy-start | bytes 2359300
  359.6 138.8 %copy-start.102 = (f32[512,96]{0,1:T(8,128)S(1)}, f32[512,96]{0,1:T(8,128)}, u32[]{:S(2)}) copy-start(f32[512,96]{0,1:T(8,128)} %param.28) | copy-start | bytes 589828
  359.6 138.8 %copy-start.103 = (f32[512,96]{0,1:T(8,128)S(1)}, f32[512,96]{0,1:T(8,128)}, u32[]{:S(2)}) copy-start(f32[512,96]{0,1:T(8,128)} %param.30) | copy-start | bytes 589828
  359.6 138.8 %copy-start.104 = (f32[512,96]{0,1:T(8,128)S(1)}, f32[512,96]{0,1:T(8,128)}, u32[]{:S(2)}) copy-start(f32[512,96]{0,1:T(8,128)} %param.29) | copy-start | bytes 589828
  359.7 116.3 %all-gather.13.cloned.1.call-start = ((), (), s32[]{:S(2)}) async-start(), calls=%async_computation.10 | async-start | bytes 1966080 | tf_op jit(solution)/shard_map/all_gather | solution.py:274
  360.2 138.2 %reduce-scatter.17.cloned.1.call-start = ((), (), s32[]{:S(2)}) async-start(), calls=%async_computation.15 | async-start | bytes 983040 | tf_op jit(solution)/shard_map/reduce_scatter | solution.py:297
  475.9 140.0 %all-gather.15.cloned.1.call-start = ((), (), s32[]{:S(2)}) async-start(), calls=%async_computation.11 | async-start | bytes 10616832 | tf_op jit(solution)/shard_map/all_gather | solution.py:280
  479.2 196.9 %all-gather.11.cloned.1.call-start = ((), (), s32[]{:S(2)}) async-start(), calls=%async_computation.9 | async-start | bytes 3538944 | tf_op jit(solution)/shard_map/all_gather | solution.py:267
  506.9 450.8 %reduce-scatter.13.cloned.1.call-start = ((), (), s32[]{:S(2)}) async-start(), calls=%async_computation.13 | async-start | bytes 14155776 | tf_op jit(solution)/shard_map/reduce_scatter | solution.py:290
  698.9 30.4 %copy-start.21 = (f32[256,768]{1,0:T(8,128)}, f32[256,768]{1,0:T(8,128)S(1)}, u32[]{:S(2)}) copy-start(f32[256,768]{1,0:T(8,128)S(1)} %get-tuple-element.190) | copy-start | bytes 2359300
  742.9 518.9 %reduce-scatter.11.cloned.1.call-start = ((), (), s32[]{:S(2)}) async-start(), calls=%async_computation.12 | async-start | bytes 21233664 | tf_op jit(solution)/shard_map/reduce_scatter | solution.py:289
  763.3 16.7 %copy-start.61 = (bf16[256,768]{0,1:T(8,128)(2,1)S(1)}, bf16[256,768]{0,1:T(8,128)(2,1)}, u32[]{:S(2)}) copy-start(bf16[256,768]{0,1:T(8,128)(2,1)} %copy.418) | copy-start | bytes 1179652
  935.0 366.7 %reduce-scatter.21.cloned.1.call-start = ((), (), s32[]{:S(2)}) async-start(), calls=%async_computation.17 | async-start | bytes 491520
  957.7 364.8 %all-reduce.3.cloned.1.call-start = ((), (), s32[]{:S(2)}) async-start(), calls=%async_computation.18 | async-start | bytes 3145728
  961.5 364.7 %reduce-scatter.19.cloned.1.call-start = ((), (), s32[]{:S(2)}) async-start(), calls=%async_computation.16 | async-start | bytes 2949120
  1292.2 29.6 %copy-start.116 = (f32[3,192]{1,0:T(4,128)S(1)}, f32[3,192]{1,0:T(4,128)}, u32[]{:S(2)}) copy-start(f32[3,192]{1,0:T(4,128)} %param.31) | copy-start | bytes 6916
  1292.2 29.6 %copy-start.121 = (f32[3,192]{1,0:T(4,128)S(1)}, f32[3,192]{1,0:T(4,128)}, u32[]{:S(2)}) copy-start(f32[3,192]{1,0:T(4,128)} %param.33) | copy-start | bytes 6916
  1292.2 29.6 %copy-start.122 = (f32[3,192]{1,0:T(4,128)S(1)}, f32[3,192]{1,0:T(4,128)}, u32[]{:S(2)}) copy-start(f32[3,192]{1,0:T(4,128)} %param.32) | copy-start | bytes 6916
  1292.2 31.3 %copy-start.75 = (f32[2,192,256]{2,1,0:T(8,128)S(1)}, f32[2,192,256]{2,1,0:T(8,128)}, u32[]{:S(2)}) copy-start(f32[2,192,256]{2,1,0:T(8,128)} %param.25) | copy-start | bytes 1179652
  (120 other events, 583.7 us)
Sparse Core Ops, SparseCore 0:
  38.9 137.5 all-gather.6
  178.5 97.6 all-gather.8
  359.7 116.0 reduce-scatter.14
  479.3 136.5 all-gather.14
  617.9 58.1 all-gather.10
  743.0 206.0 reduce-scatter.12
  953.0 308.7 reduce-scatter.10
  1264.9 19.9 reduce-scatter.20
  1287.4 32.7 reduce-scatter.18
Sparse Core Ops, SparseCore 1:
  362.3 17.6 all-gather.12
  476.0 22.4 reduce-scatter.16
  961.5 42.5 all-reduce.2
